TPU v7x, 32 devices: a whole 2x2x4 slice. The times are simulated.
32 devices in a mesh: dp: 8 (over z, x), fsdp: 4 (over y, core).
Axes of the slice: x: 2, y: 2, z: 4, core: 2. Of those that a mesh axis runs over, the one named last changes fastest.
Arguments:
- tokens: bfloat16 [16384, 640], P(('dp', 'fsdp')), may hold values from -6 to 6
- cotangent: bfloat16 [16384, 640], P(('dp', 'fsdp')), may hold values from -6 to 6
- segments: int32 [64, 256], P(('dp', 'fsdp')), may hold values from 0 to 7, never falling along the last dimension, each value on 1 to 128 neighbouring positions
- query_weight: float32 [1024, 640], P(('dp', 'fsdp')), may hold values from -0.25 to 0.25
- key_weight: float32 [640, 256], P(('dp', 'fsdp')), may hold values from -0.25 to 0.25
- value_weight: float32 [640, 256], P(('dp', 'fsdp')), may hold values from -0.25 to 0.25
- out_weight: float32 [1024, 640], P(('dp', 'fsdp')), may hold values from -0.1875 to 0.1875
- gate_weight: float32 [2048, 640], P(('dp', 'fsdp')), may hold values from -0.25 to 0.25
- up_weight: float32 [2048, 640], P(('dp', 'fsdp')), may hold values from -0.25 to 0.25
- down_weight: float32 [2048, 640], P(('dp', 'fsdp')), may hold values from -0.125 to 0.125
- norm_gains: float32 [3072], P(('dp', 'fsdp')), may hold values from 0.5 to 1.5
- query_state: float32 [1024, 640], P(('dp', 'fsdp')), may hold values from -224 to 224
- key_state: float32 [640, 256], P(('dp', 'fsdp')), may hold values from -224 to 224
- value_state: float32 [640, 256], P(('dp', 'fsdp')), may hold values from -224 to 224
- out_state: float32 [1024, 640], P(('dp', 'fsdp')), may hold values from -224 to 224
- gate_state: float32 [2048, 640], P(('dp', 'fsdp')), may hold values from -224 to 224
- up_state: float32 [2048, 640], P(('dp', 'fsdp')), may hold values from -224 to 224
- down_state: float32 [2048, 640], P(('dp', 'fsdp')), may hold values from -224 to 224
- gains_state: float32 [3072], P(('dp', 'fsdp')), may hold values from -224 to 224
Outputs:
- block_out: bfloat16 [16384, 640], P(('dp', 'fsdp'))
- tokens_grad: bfloat16 [16384, 640], P(('dp', 'fsdp'))
- query_grad: float32 [1024, 640], P(('dp', 'fsdp'))
- key_grad: float32 [640, 256], P(('dp', 'fsdp'))
- value_grad: float32 [640, 256], P(('dp', 'fsdp'))
- out_grad: float32 [1024, 640], P(('dp', 'fsdp'))
- gate_grad: float32 [2048, 640], P(('dp', 'fsdp'))
- up_grad: float32 [2048, 640], P(('dp', 'fsdp'))
- down_grad: float32 [2048, 640], P(('dp', 'fsdp'))
- gains_grad: float32 [3072], P(('dp', 'fsdp'))
- query_new: float32 [1024, 640], P(('dp', 'fsdp'))
- key_new: float32 [640, 256], P(('dp', 'fsdp'))
- value_new: float32 [640, 256], P(('dp', 'fsdp'))
- out_new: float32 [1024, 640], P(('dp', 'fsdp'))
- gate_new: float32 [2048, 640], P(('dp', 'fsdp'))
- up_new: float32 [2048, 640], P(('dp', 'fsdp'))
- down_new: float32 [2048, 640], P(('dp', 'fsdp'))
- gains_new: float32 [3072], P(('dp', 'fsdp'))
- query_moment: float32 [1024, 640], P(('dp', 'fsdp'))
- key_moment: float32 [640, 256], P(('dp', 'fsdp'))
- value_moment: float32 [640, 256], P(('dp', 'fsdp'))
- out_moment: float32 [1024, 640], P(('dp', 'fsdp'))
- gate_moment: float32 [2048, 640], P(('dp', 'fsdp'))
- up_moment: float32 [2048, 640], P(('dp', 'fsdp'))
- down_moment: float32 [2048, 640], P(('dp', 'fsdp'))
- gains_moment: float32 [3072], P(('dp', 'fsdp'))
Inputs may be any that keep to these rules, and one draw needn't show every extreme that they name: `segments`: segment numbers never fall along a row; the tokens of one number form one sequence.
All inputs are finite; a program needn't handle non-finite values.
Results may differ from a plain program's by a relative error of at most 0.015.
The roundings to bfloat16 on the way count: a program that leaves them out, or rounds other values in their place, can miss the bound.
Values may be sent and summed in bfloat16 or wider, within the bound.
A program may use at most 320 MiB of HBM per device.

v0:
```python
import math

import jax
import jax.numpy as jnp
from jax import lax
from jax.sharding import PartitionSpec as P

D = 640
HEADS = 4
HD = 256
FF = 2048
NS_ITERS = 5


EPSILON = 1e-06
THETA = 1000000.0
MOMENTUM = 0.95
LEARN_RATE = 0.05
NS_FIRST = 3.4445
NS_SECOND = -4.775
NS_THIRD = 2.0315
HIGHEST = lax.Precision.HIGHEST
MASKED = -1e30


def dot_plain(left, right):
    return jnp.dot(left, right, preferred_element_type=jnp.float32)


def dot_right_t(left, right):
    return lax.dot_general(
        left, right, (((1,), (1,)), ((), ())), preferred_element_type=jnp.float32
    )


def dot_left_t(left, right):
    return lax.dot_general(
        left, right, (((0,), (0,)), ((), ())), preferred_element_type=jnp.float32
    )


def norm_rows(values, gain):
    return values * lax.rsqrt(jnp.mean(values * values, axis=-1, keepdims=True) + EPSILON) * gain


def rotary(values, cosine, sine):
    middle = values.shape[-1] // 2
    first_half = values[..., :middle]
    second_half = values[..., middle:]
    return jnp.concatenate(
        [first_half * cosine - second_half * sine, second_half * cosine + first_half * sine],
        axis=-1,
    )


def rotary_tables(segment, head_size):
    length = segment.shape[0]
    starts = jnp.sum((segment[None, :] < segment[:, None]).astype(jnp.int32), axis=1)
    places = (jnp.arange(length, dtype=jnp.int32) - starts).astype(jnp.float32)
    frequency = jnp.exp(
        -math.log(THETA) * 2.0 * jnp.arange(head_size // 2, dtype=jnp.float32) / head_size
    )
    angles = places[:, None] * frequency[None, :]
    return (jnp.cos(angles), jnp.sin(angles))


def allowed_pairs(segment):
    length = segment.shape[0]
    positions = jnp.arange(length, dtype=jnp.int32)
    same_doc = segment[:, None] == segment[None, :]
    return jnp.logical_and(same_doc, positions[None, :] <= positions[:, None])


def split_gains(gain_vec, width, head_size):
    return (
        gain_vec[:width],
        gain_vec[width : 2 * width],
        gain_vec[2 * width : 3 * width],
        gain_vec[3 * width : 4 * width],
        gain_vec[4 * width : 4 * width + head_size],
        gain_vec[4 * width + head_size :],
    )


def query_rotated(query, gain, cosine, sine):
    length = query.shape[0]
    shaped = query.reshape(length, HEADS, query.shape[1] // HEADS)
    return rotary(norm_rows(shaped, gain), cosine[:, None, :], sine[:, None, :])


def key_rotated(key_rows, gain, cosine, sine):
    return rotary(norm_rows(key_rows, gain), cosine, sine)


def attention_scores(query_bf, key_bf, allowed):
    scale = query_bf.shape[-1] ** (-0.5)
    products = (
        jnp.einsum("thd,sd->hts", query_bf, key_bf, preferred_element_type=jnp.float32) * scale
    )
    return jnp.where(allowed[None], products, MASKED)


def gelu_product(gate, upward):
    return jax.nn.gelu(gate, approximate=True) * upward


def forward(rows_in, segment, weights, gain_vec):
    query_w, key_w, value_w, out_w, gate_w, up_w, down_w = weights
    width = rows_in.shape[1]
    head_size = key_w.shape[1]
    gain_in, gain_attn, gain_ff, gain_post, gain_query, gain_key = split_gains(
        gain_vec, width, head_size
    )
    x_rows = rows_in.astype(jnp.float32)
    normed = norm_rows(x_rows, gain_in).astype(jnp.bfloat16)
    query = dot_right_t(normed, query_w)
    key_rows = dot_plain(normed, key_w)
    value = dot_plain(normed, value_w).astype(jnp.bfloat16)
    cosine, sine = rotary_tables(segment, head_size)
    query_bf = query_rotated(query, gain_query, cosine, sine).astype(jnp.bfloat16)
    key_bf = key_rotated(key_rows, gain_key, cosine, sine).astype(jnp.bfloat16)
    allowed = allowed_pairs(segment)
    scores = attention_scores(query_bf, key_bf, allowed)
    peak = jnp.max(scores, axis=-1, keepdims=True)
    log_total = peak + jnp.log(jnp.sum(jnp.exp(scores - peak), axis=-1, keepdims=True))
    probs = jnp.exp(scores - log_total).astype(jnp.bfloat16)
    mixed = jnp.einsum("hts,sd->thd", probs, value, preferred_element_type=jnp.float32)
    mixed = mixed.astype(jnp.bfloat16).reshape(rows_in.shape[0], -1)
    attn = dot_plain(mixed, out_w)
    hidden = x_rows + norm_rows(attn, gain_attn)
    ff_in = norm_rows(hidden, gain_ff).astype(jnp.bfloat16)
    gate = dot_right_t(ff_in, gate_w)
    upward = dot_right_t(ff_in, up_w)
    act = gelu_product(gate, upward).astype(jnp.bfloat16)
    ff_out = dot_plain(act, down_w)
    result = (hidden + norm_rows(ff_out, gain_post)).astype(jnp.bfloat16)
    saved = (
        x_rows,
        normed,
        query,
        key_rows,
        value,
        query_bf,
        key_bf,
        allowed,
        cosine,
        sine,
        log_total,
        mixed,
        attn,
        hidden,
        ff_in,
        gate,
        upward,
        act,
        ff_out,
    )
    return (result, saved)


def backward(saved, cot_rows, weights, gain_vec):
    (
        x_rows,
        normed,
        query,
        key_rows,
        value,
        query_bf,
        key_bf,
        allowed,
        cosine,
        sine,
        log_total,
        mixed,
        attn,
        hidden,
        ff_in,
        gate,
        upward,
        act,
        ff_out,
    ) = saved
    query_w, key_w, value_w, out_w, gate_w, up_w, down_w = weights
    width = x_rows.shape[1]
    head_size = key_w.shape[1]
    gain_in, gain_attn, gain_ff, gain_post, gain_query, gain_key = split_gains(
        gain_vec, width, head_size
    )
    d_output = cot_rows.astype(jnp.float32)
    unused, pullback = jax.vjp(norm_rows, ff_out, gain_post)
    d_ffout, dg_post = pullback(d_output)
    d_ffout = d_ffout.astype(jnp.bfloat16)
    down_grad = dot_left_t(act, d_ffout)
    d_act = dot_right_t(d_ffout, down_w)
    unused, pullback = jax.vjp(gelu_product, gate, upward)
    d_gate, d_upward = pullback(d_act)
    d_gate = d_gate.astype(jnp.bfloat16)
    d_upward = d_upward.astype(jnp.bfloat16)
    gate_grad = dot_left_t(d_gate, ff_in)
    up_grad = dot_left_t(d_upward, ff_in)
    d_ffin = dot_plain(d_gate, gate_w) + dot_plain(d_upward, up_w)
    unused, pullback = jax.vjp(norm_rows, hidden, gain_ff)
    d_inner, dg_ff = pullback(d_ffin)
    d_hidden = d_output + d_inner
    unused, pullback = jax.vjp(norm_rows, attn, gain_attn)
    d_attn, dg_attn = pullback(d_hidden)
    d_attn = d_attn.astype(jnp.bfloat16)
    out_grad = dot_left_t(mixed, d_attn)
    d_mixed = (
        dot_right_t(d_attn, out_w).astype(jnp.bfloat16).reshape(x_rows.shape[0], HEADS, head_size)
    )
    scores = attention_scores(query_bf, key_bf, allowed)
    probs_full = jnp.exp(scores - log_total)
    probs = probs_full.astype(jnp.bfloat16)
    d_value = jnp.einsum("hts,thd->sd", probs, d_mixed, preferred_element_type=jnp.float32).astype(
        jnp.bfloat16
    )
    d_probs = jnp.einsum("thd,sd->hts", d_mixed, value, preferred_element_type=jnp.float32)
    row_dot = jnp.sum(probs_full * d_probs, axis=-1, keepdims=True)
    d_scores = (probs_full * (d_probs - row_dot) * head_size ** (-0.5)).astype(jnp.bfloat16)
    d_qrot = jnp.einsum("hts,sd->thd", d_scores, key_bf, preferred_element_type=jnp.float32)
    d_krot = jnp.einsum("hts,thd->sd", d_scores, query_bf, preferred_element_type=jnp.float32)
    unused, pullback = jax.vjp(
        lambda values, gain: query_rotated(values, gain, cosine, sine), query, gain_query
    )
    d_query, dg_query = pullback(d_qrot)
    unused, pullback = jax.vjp(
        lambda values, gain: key_rotated(values, gain, cosine, sine), key_rows, gain_key
    )
    d_key, dg_key = pullback(d_krot)
    d_query = d_query.astype(jnp.bfloat16)
    d_key = d_key.astype(jnp.bfloat16)
    query_grad = dot_left_t(d_query, normed)
    key_grad = dot_left_t(normed, d_key)
    value_grad = dot_left_t(normed, d_value)
    d_normed = (
        dot_plain(d_query, query_w) + dot_right_t(d_key, key_w) + dot_right_t(d_value, value_w)
    )
    unused, pullback = jax.vjp(norm_rows, x_rows, gain_in)
    d_inputs, dg_in = pullback(d_normed)
    grad_rows = (d_hidden + d_inputs).astype(jnp.bfloat16)
    gain_grad = jnp.concatenate([dg_in, dg_attn, dg_ff, dg_post, dg_query, dg_key])
    grads = (query_grad, key_grad, value_grad, out_grad, gate_grad, up_grad, down_grad)
    return (grad_rows, grads, gain_grad)


def whole_weights(fetched):
    weights = tuple((fetched[number].reshape(-1, fetched[number].shape[-1]) for number in range(7)))
    return (weights, fetched[7].reshape(-1).astype(jnp.float32))


def fetch_forward(parts):
    fetched = (
        lax.all_gather(parts[0][:, None], "fsdp", axis=1, tiled=True),
        lax.all_gather(parts[1][:, None], "fsdp", axis=1, tiled=True),
        lax.all_gather(parts[2][:, None], "fsdp", axis=1, tiled=True),
        lax.all_gather(parts[3][:, None], "fsdp", axis=1, tiled=True),
        lax.all_gather(parts[4][:, None], "fsdp", axis=1, tiled=True),
        lax.all_gather(parts[5][:, None], "fsdp", axis=1, tiled=True),
        lax.all_gather(parts[6][:, None], "fsdp", axis=1, tiled=True),
        lax.all_gather(parts[7][:, None], "fsdp", axis=1, tiled=True),
    )
    return whole_weights(fetched)


def fetch_backward(parts):
    fetched = (
        lax.all_gather(parts[0][:, None], "fsdp", axis=1, tiled=True),
        lax.all_gather(parts[1][:, None], "fsdp", axis=1, tiled=True),
        lax.all_gather(parts[2][:, None], "fsdp", axis=1, tiled=True),
        lax.all_gather(parts[3][:, None], "fsdp", axis=1, tiled=True),
        lax.all_gather(parts[4][:, None], "fsdp", axis=1, tiled=True),
        lax.all_gather(parts[5][:, None], "fsdp", axis=1, tiled=True),
        lax.all_gather(parts[6][:, None], "fsdp", axis=1, tiled=True),
        lax.all_gather(parts[7][:, None], "fsdp", axis=1, tiled=True),
    )
    return whole_weights(fetched)


def newton_step(iterate, gram_matrix):
    polynomial = NS_SECOND * gram_matrix + NS_THIRD * jnp.einsum(
        "kij,kjl->kil",
        gram_matrix,
        gram_matrix,
        precision=HIGHEST,
        preferred_element_type=jnp.float32,
    )
    return NS_FIRST * iterate + jnp.einsum(
        "kri,kil->krl", iterate, polynomial, precision=HIGHEST, preferred_element_type=jnp.float32
    )


def shards(
    tokens,
    cotangent,
    segments,
    query_weight,
    key_weight,
    value_weight,
    out_weight,
    gate_weight,
    up_weight,
    down_weight,
    norm_gains,
    query_state,
    key_state,
    value_state,
    out_state,
    gate_state,
    up_state,
    down_state,
    gains_state,
):
    lanes = lax.axis_size("fsdp")
    groups = lax.axis_size("dp")
    devices_all = lanes * groups
    slots = (lanes + 6) // lanes
    total_slots = lanes * slots
    owners = jnp.array([number * total_slots // 7 for number in range(7)], jnp.int32)
    my_group = lax.axis_index("dp")
    my_lane = lax.axis_index("fsdp")
    my_device = my_group * lanes + my_lane
    masters = (
        query_weight,
        key_weight,
        value_weight,
        out_weight,
        gate_weight,
        up_weight,
        down_weight,
    )
    states = (query_state, key_state, value_state, out_state, gate_state, up_state, down_state)
    query_part = query_weight.astype(jnp.bfloat16)[None]
    key_part = key_weight.astype(jnp.bfloat16)[None]
    value_part = value_weight.astype(jnp.bfloat16)[None]
    out_part = out_weight.astype(jnp.bfloat16)[None]
    gate_part = gate_weight.astype(jnp.bfloat16)[None]
    up_part = up_weight.astype(jnp.bfloat16)[None]
    down_part = down_weight.astype(jnp.bfloat16)[None]
    gains_part = norm_gains.astype(jnp.bfloat16)[None]
    group_parts = (
        lax.all_gather(query_part, "dp", axis=0, tiled=True),
        lax.all_gather(key_part, "dp", axis=0, tiled=True),
        lax.all_gather(value_part, "dp", axis=0, tiled=True),
        lax.all_gather(out_part, "dp", axis=0, tiled=True),
        lax.all_gather(gate_part, "dp", axis=0, tiled=True),
        lax.all_gather(up_part, "dp", axis=0, tiled=True),
        lax.all_gather(down_part, "dp", axis=0, tiled=True),
        lax.all_gather(gains_part, "dp", axis=0, tiled=True),
    )
    batches = segments.shape[0]
    capacity = tokens.shape[0] // batches
    grad_sums = [
        jnp.zeros((matrix.shape[0] * devices_all, matrix.shape[1]), jnp.float32)
        for matrix in masters
    ]
    gain_total = jnp.zeros((norm_gains.shape[0] * devices_all,), jnp.float32)
    results = []
    grad_outputs = []
    for batch in range(batches):
        rows_in = tokens[batch * capacity : (batch + 1) * capacity]
        cot_rows = cotangent[batch * capacity : (batch + 1) * capacity]
        weights_now, gains_now = fetch_forward(group_parts)
        result, saved = forward(rows_in, segments[batch], weights_now, gains_now)
        back_weights, back_gains = fetch_backward(group_parts)
        grad_rows, grads, gain_grad = backward(saved, cot_rows, back_weights, back_gains)
        grad_sums = [total + extra for total, extra in zip(grad_sums, grads)]
        gain_total = gain_total + gain_grad
        results.append(result)
        grad_outputs.append(grad_rows)
    block_out = jnp.concatenate(results, axis=0)
    tokens_grad = jnp.concatenate(grad_outputs, axis=0)
    slot_ids = jnp.arange(total_slots, dtype=jnp.int32)
    matches = (owners[None, :] == slot_ids[:, None]).astype(jnp.int32)
    holder = jnp.sum(matches * jnp.arange(7, dtype=jnp.int32)[None, :], axis=1) + 7 * (
        1 - jnp.sum(matches, axis=1)
    )
    tile_rows = FF // groups
    per_rows = FF // devices_all
    row_table = jnp.array(
        [
            HEADS * HD // devices_all,
            D // devices_all,
            D // devices_all,
            HEADS * HD // devices_all,
            FF // devices_all,
            FF // devices_all,
            FF // devices_all,
            0,
        ],
        jnp.int32,
    )
    shares = []
    for place in range(slots):
        matrix_id = holder[my_lane * slots + place]
        shares.append(jnp.sum(jnp.where(jnp.arange(8, dtype=jnp.int32) == matrix_id, row_table, 0)))
    padded = []
    for number in range(7):
        grad_full = grad_sums[number]
        own_rows = states[number].shape[0]
        start_row = my_device * own_rows
        current = lax.dynamic_slice_in_dim(grad_full, start_row, own_rows, 0)
        grad_full = lax.dynamic_update_slice_in_dim(
            grad_full, current + MOMENTUM * states[number], start_row, 0
        )
        blocked = grad_full.reshape(groups, grad_full.shape[0] // groups, grad_full.shape[1])
        padded.append(
            jnp.pad(blocked, ((0, 0), (0, tile_rows - blocked.shape[1]), (0, D - blocked.shape[2])))
        )
    padded.append(jnp.zeros((groups, tile_rows, D), jnp.float32))
    stacked = jnp.stack(padded, axis=1)
    routed = jnp.take(stacked, holder, axis=1).reshape(devices_all, slots, tile_rows, D)
    gain_rows = norm_gains.shape[0]
    gain_start = my_device * gain_rows
    gain_current = lax.dynamic_slice_in_dim(gain_total, gain_start, gain_rows, 0)
    gain_total = lax.dynamic_update_slice_in_dim(
        gain_total, gain_current + MOMENTUM * gains_state, gain_start, 0
    )
    gain_routed = gain_total.reshape(devices_all, gain_rows)
    owned, gain_owned = (
        lax.psum_scatter(routed, ("dp", "fsdp"), scatter_dimension=0, tiled=True),
        lax.psum_scatter(gain_routed, ("dp", "fsdp"), scatter_dimension=0, tiled=True),
    )
    moment_tile = owned[0]
    gains_moment = gain_owned[0]
    whole_tile = lax.all_gather(moment_tile.astype(jnp.bfloat16), "dp", axis=1, tiled=True).astype(
        moment_tile.dtype
    )
    inverse = 1.0 / (jnp.sqrt(jnp.sum(whole_tile * whole_tile, axis=(1, 2))) + 1e-07)
    iterate = whole_tile * inverse[:, None, None]
    for iteration in range(NS_ITERS):
        gram_matrix = jnp.einsum(
            "kri,krj->kij", iterate, iterate, precision=HIGHEST, preferred_element_type=jnp.float32
        )
        iterate = newton_step(iterate, gram_matrix)
    ortho_tile = lax.dynamic_slice_in_dim(iterate, my_group * tile_rows, tile_rows, 1)
    lane_ids = jnp.arange(lanes, dtype=jnp.int32)
    offsets = jnp.arange(per_rows, dtype=jnp.int32)
    ortho_pieces = []
    moment_pieces = []
    for place in range(slots):
        picks = jnp.minimum(
            lane_ids[:, None] * shares[place] + offsets[None, :], tile_rows - 1
        ).reshape(-1)
        ortho_pieces.append(jnp.take(ortho_tile[place], picks, axis=0).reshape(lanes, per_rows, D))
        moment_pieces.append(
            jnp.take(moment_tile[place], picks, axis=0).reshape(lanes, per_rows, D)
        )
    ortho_send = jnp.stack(ortho_pieces, axis=1)
    moment_send = jnp.stack(moment_pieces, axis=1)
    ortho_back, moment_back = (
        lax.all_to_all(
            ortho_send.astype(jnp.bfloat16), "fsdp", split_axis=0, concat_axis=0, tiled=True
        ).astype(ortho_send.dtype),
        lax.all_to_all(
            moment_send.astype(jnp.bfloat16), "fsdp", split_axis=0, concat_axis=0, tiled=True
        ).astype(moment_send.dtype),
    )
    grad_list = []
    updated = []
    moments = []
    for number in range(7):
        lane_slot = owners[number]
        source_lane = lane_slot // slots
        source_place = lane_slot % slots
        rows_here, cols_here = masters[number].shape
        got_ortho = lax.dynamic_index_in_dim(
            lax.dynamic_index_in_dim(ortho_back, source_lane, 0, keepdims=False),
            source_place,
            0,
            keepdims=False,
        )[:rows_here, :cols_here]
        got_moment = lax.dynamic_index_in_dim(
            lax.dynamic_index_in_dim(moment_back, source_lane, 0, keepdims=False),
            source_place,
            0,
            keepdims=False,
        )[:rows_here, :cols_here]
        factor = LEARN_RATE * 0.2 * math.sqrt(max(rows_here * devices_all, cols_here))
        updated.append(masters[number] - factor * got_ortho)
        moments.append(got_moment)
        grad_list.append(got_moment - MOMENTUM * states[number])
    gains_grad = gains_moment - MOMENTUM * gains_state
    tokens_all = tokens.shape[0] * devices_all
    gains_new = norm_gains - 0.1 / math.sqrt(tokens_all) * gains_moment
    return (
        block_out,
        tokens_grad,
        grad_list[0],
        grad_list[1],
        grad_list[2],
        grad_list[3],
        grad_list[4],
        grad_list[5],
        grad_list[6],
        gains_grad,
        updated[0],
        updated[1],
        updated[2],
        updated[3],
        updated[4],
        updated[5],
        updated[6],
        gains_new,
        moments[0],
        moments[1],
        moments[2],
        moments[3],
        moments[4],
        moments[5],
        moments[6],
        gains_moment,
    )


def solution(mesh):
    return jax.shard_map(
        shards,
        mesh=mesh,
        in_specs=(
            P(("dp", "fsdp"), None),
            P(("dp", "fsdp"), None),
            P(("dp", "fsdp"), None),
            P(("dp", "fsdp"), None),
            P(("dp", "fsdp"), None),
            P(("dp", "fsdp"), None),
            P(("dp", "fsdp"), None),
            P(("dp", "fsdp"), None),
            P(("dp", "fsdp"), None),
            P(("dp", "fsdp"), None),
            P(("dp", "fsdp")),
            P(("dp", "fsdp"), None),
            P(("dp", "fsdp"), None),
            P(("dp", "fsdp"), None),
            P(("dp", "fsdp"), None),
            P(("dp", "fsdp"), None),
            P(("dp", "fsdp"), None),
            P(("dp", "fsdp"), None),
            P(("dp", "fsdp")),
        ),
        out_specs=(
            P(("dp", "fsdp"), None),
            P(("dp", "fsdp"), None),
            P(("dp", "fsdp"), None),
            P(("dp", "fsdp"), None),
            P(("dp", "fsdp"), None),
            P(("dp", "fsdp"), None),
            P(("dp", "fsdp"), None),
            P(("dp", "fsdp"), None),
            P(("dp", "fsdp"), None),
            P(("dp", "fsdp")),
            P(("dp", "fsdp"), None),
            P(("dp", "fsdp"), None),
            P(("dp", "fsdp"), None),
            P(("dp", "fsdp"), None),
            P(("dp", "fsdp"), None),
            P(("dp", "fsdp"), None),
            P(("dp", "fsdp"), None),
            P(("dp", "fsdp")),
            P(("dp", "fsdp"), None),
            P(("dp", "fsdp"), None),
            P(("dp", "fsdp"), None),
            P(("dp", "fsdp"), None),
            P(("dp", "fsdp"), None),
            P(("dp", "fsdp"), None),
            P(("dp", "fsdp"), None),
            P(("dp", "fsdp")),
        ),
        check_vma=False,
    )
```

profile of v0, /device:TPU:26, one launch (start us, length us, event | category | flops | bytes accessed | tf_op | source)
XLA Modules:
  0.0 1510.7 jit_solution(14397038182156091521)
XLA Ops:
  8.3 33.0 %all-gather.6 = bf16[256,640]{1,0:T(8,128)(2,1)} all-gather(bf16[32,640]{1,0:T(8,128)(2,1)S(1)} %convert_element_type.223), channel_id=8, replica_groups=mesh['dp'=8,'fsdp'=4] {'dp'}, dimensions={0}, use_global_device_ids=true | all-gather | bytes 368640 | tf_op jit(solution)/shard_map/all_gather | solution.py:342
  42.3 33.0 %all-gather.8 = bf16[256,640]{1,0:T(8,128)(2,1)} all-gather(bf16[32,640]{1,0:T(8,128)(2,1)S(1)} %convert_element_type.227), channel_id=10, replica_groups=mesh['dp'=8,'fsdp'=4] {'dp'}, dimensions={0}, use_global_device_ids=true | all-gather | bytes 368640 | tf_op jit(solution)/shard_map/all_gather | solution.py:345
  76.4 33.9 %all-gather.10 = bf16[512,640]{1,0:T(8,128)(2,1)} all-gather(bf16[64,640]{1,0:T(8,128)(2,1)S(1)} %convert_element_type.229), channel_id=12, replica_groups=mesh['dp'=8,'fsdp'=4] {'dp'}, dimensions={0}, use_global_device_ids=true | all-gather | bytes 737280 | tf_op jit(solution)/shard_map/all_gather | solution.py:346
  110.4 34.2 %all-gather.12 = bf16[512,640]{1,0:T(8,128)(2,1)} all-gather(bf16[64,640]{1,0:T(8,128)(2,1)S(1)} %convert_element_type.230), channel_id=14, replica_groups=mesh['dp'=8,'fsdp'=4] {'dp'}, dimensions={0}, use_global_device_ids=true | all-gather | bytes 737280 | tf_op jit(solution)/shard_map/all_gather | solution.py:347
  144.7 33.4 %all-gather.14 = bf16[512,640]{1,0:T(8,128)(2,1)} all-gather(bf16[64,640]{1,0:T(8,128)(2,1)S(1)} %convert_element_type.232), channel_id=16, replica_groups=mesh['dp'=8,'fsdp'=4] {'dp'}, dimensions={0}, use_global_device_ids=true | all-gather | bytes 737280 | tf_op jit(solution)/shard_map/all_gather | solution.py:348
  203.1 30.6 %all-gather.18 = bf16[8,20,256]{2,1,0:T(8,128)(2,1)S(1)} all-gather(bf16[1,20,256]{2,1,0:T(8,128)(2,1)S(1)} %convert_bitcast_fusion.1), channel_id=4, replica_groups=mesh['dp'=8,'fsdp'=4] {'dp'}, dimensions={0}, use_global_device_ids=true | all-gather | bytes 92160 | tf_op jit(solution)/shard_map/all_gather | solution.py:344
  240.2 30.6 %all-gather.19 = bf16[8,20,256]{2,1,0:T(8,128)(2,1)S(1)} all-gather(bf16[1,20,256]{2,1,0:T(8,128)(2,1)S(1)} %convert_bitcast_fusion), channel_id=6, replica_groups=mesh['dp'=8,'fsdp'=4] {'dp'}, dimensions={0}, use_global_device_ids=true | all-gather | bytes 92160 | tf_op jit(solution)/shard_map/all_gather | solution.py:343
  424.7 17.5 %mini-gather-slice.2 = f32[8,8,256,384]{3,2,0,1:T(8,128)} slice(f32[8,8,256,640]{3,2,0,1:T(8,128)} %broadcast_dynamic-update-slice_fusion), slice={[0:8], [0:8], [0:256], [0:384]} | slice | bytes 50331648 | tf_op jit(solution)/shard_map/jit(_take)/gather | solution.py:412
  456.5 18.7 %gather_fusion = f32[8,8,256,384]{3,2,1,0:T(8,128)} fusion(f32[8,8,256,384]{3,2,0,1:T(8,128)} %mini-gather-slice.2, s32[1024]{0:T(1024)} %pad_clamp_fusion.2), kind=kCustom, calls=%fused_computation.4 | custom fusion | bytes 50331680 | tf_op jit(solution)/shard_map/jit(_take)/gather | solution.py:412
  475.2 28.4 %pad_maximum_fusion = f32[8,8,256,640]{3,2,0,1:T(8,128)} fusion(f32[8,8,256,256]{3,2,0,1:T(8,128)} %bitcast.310, f32[8,8,256,384]{3,2,0,1:T(8,128)} %bitcast.309), kind=kLoop, calls=%fused_computation.8 | loop fusion | flops 10485760 | bytes 83886080
  503.6 29.2 %copy.233 = f32[8,8,256,640]{3,2,1,0:T(8,128)} copy(f32[8,8,256,640]{3,2,0,1:T(8,128)} %pad_maximum_fusion) | data formatting | bytes 83886080
  532.8 29.5 %broadcast_select_fusion = f32[32,2,256,640]{3,2,1,0:T(8,128)} fusion(f32[32,2,256,640]{3,2,1,0:T(8,128)} %bitcast.308, pred[32,2]{1,0:T(8,128)(4,1)S(1)} %bitcast.371), kind=kLoop, calls=%fused_computation.9 | loop fusion | flops 10485760 | bytes 83886144 | tf_op jit(solution)/shard_map/jit(_take)/select_n | solution.py:412
  562.5 440.5 %reduce-scatter.2.cloned.1.call-done = f32[1,2,256,640]{3,2,1,0:T(8,128)} async-done(((f32[32,2,256,640]{3,2,1,0:T(8,128)}), f32[1,2,256,640]{3,2,1,0:T(8,128)}) %reduce-scatter.2.cloned.1.call-update) | async-done | bytes 1310736 | tf_op jit(solution)/shard_map/reduce_scatter | solution.py:421
  1035.1 49.1 %all-reduce.13 = f32[32,96]{1,0:T(8,128)S(1)} all-reduce(f32[32,96]{1,0:T(8,128)S(1)} %reshape.741), channel_id=20, replica_groups=mesh['dp'=8,'fsdp'=4] {'dp','fsdp'}, use_global_device_ids=true, to_apply=%region_49.0.clone | all-reduce | flops 3072 | bytes 24576
  1099.2 28.9 %fusion.3 = f32[2,640,640]{2,1,0:T(8,128)S(1)} fusion(bf16[1,2,2048,640]{3,2,1,0:T(8,128)(2,1)S(1)} %copy-done.31, f32[2]{0:T(128)S(1)} %add_divide_fusion), kind=kOutput, calls=%fused_computation.13 | convolution fusion | flops 20137902080 | bytes 8519688 | tf_op jit(solution)/shard_map/kri,krj->kij/dot_general | solution.py:432
  1137.6 33.2 %fusion.5 = f32[2,2048,640]{2,1,0:T(8,128)S(1)} fusion(bf16[1,2,2048,640]{3,2,1,0:T(8,128)(2,1)S(1)} %copy-done.31, f32[2]{0:T(128)S(1)} %add_divide_fusion, f32[2,640,640]{2,1,0:T(8,128)S(1)} %fusion.252, f32[2,640,640]{2,1,0:T(8,128)S(1)} %fusion.3), kind=kOutput, calls=%fused_computation.15 | convolution fusion | flops 20150845440 | bytes 22282248 | tf_op jit(solution)/shard_map/kri,kil->krl/dot_general | solution.py:288
  1170.8 28.6 %fusion.253 = f32[2,640,640]{2,1,0:T(8,128)S(1)} fusion(f32[2,2048,640]{2,1,0:T(8,128)S(1)} %fusion.5), kind=kOutput, calls=%fused_computation.486 | convolution fusion | flops 20132659200 | bytes 13762560 | tf_op jit(solution)/shard_map/kri,krj->kij/dot_general | solution.py:432
  1210.6 34.0 %multiply_add_fusion.2 = f32[2,2048,640]{2,1,0:T(8,128)S(1)} fusion(f32[2,2048,640]{2,1,0:T(8,128)S(1)} %fusion.5, f32[2,640,640]{2,1,0:T(8,128)S(1)} %fusion.254, f32[2,640,640]{2,1,0:T(8,128)} %copy-done.1), kind=kOutput, calls=%fused_computation.19 | convolution fusion | flops 20140359680 | bytes 27525120 | tf_op jit(solution)/shard_map/kri,kil->krl/dot_general | solution.py:288
  1244.5 28.4 %fusion.255 = f32[2,640,640]{2,1,0:T(8,128)S(1)} fusion(f32[2,2048,640]{2,1,0:T(8,128)S(1)} %multiply_add_fusion.2), kind=kOutput, calls=%fused_computation.488 | convolution fusion | flops 20132659200 | bytes 13762560 | tf_op jit(solution)/shard_map/kri,krj->kij/dot_general | solution.py:432
  1284.1 34.0 %multiply_add_fusion.1 = f32[2,2048,640]{2,1,0:T(8,128)S(1)} fusion(f32[2,2048,640]{2,1,0:T(8,128)S(1)} %multiply_add_fusion.2, f32[2,640,640]{2,1,0:T(8,128)S(1)} %fusion.256, f32[2,640,640]{2,1,0:T(8,128)} %copy-done.2), kind=kOutput, calls=%fused_computation.18 | convolution fusion | flops 20140359680 | bytes 27525120 | tf_op jit(solution)/shard_map/kri,kil->krl/dot_general | solution.py:288
  1318.1 28.6 %fusion.257 = f32[2,640,640]{2,1,0:T(8,128)S(1)} fusion(f32[2,2048,640]{2,1,0:T(8,128)S(1)} %multiply_add_fusion.1), kind=kOutput, calls=%fused_computation.490 | convolution fusion | flops 20132659200 | bytes 13762560 | tf_op jit(solution)/shard_map/kri,krj->kij/dot_general | solution.py:432
  1356.1 34.2 %multiply_add_fusion = f32[2,2048,640]{2,1,0:T(8,128)S(1)} fusion(f32[2,2048,640]{2,1,0:T(8,128)} %copy-done, f32[2,640,640]{2,1,0:T(8,128)S(1)} %fusion.258, f32[2,640,640]{2,1,0:T(8,128)S(1)} %fusion.257), kind=kOutput, calls=%fused_computation.17 | convolution fusion | flops 20140359680 | bytes 27525120 | tf_op jit(solution)/shard_map/kri,kil->krl/dot_general | solution.py:288
  1390.4 28.8 %fusion.259 = f32[2,640,640]{2,1,0:T(8,128)S(1)} fusion(f32[2,2048,640]{2,1,0:T(8,128)S(1)} %multiply_add_fusion), kind=kOutput, calls=%fused_computation.492 | convolution fusion | flops 20132659200 | bytes 13762560 | tf_op jit(solution)/shard_map/kri,krj->kij/dot_general | solution.py:432
  1428.6 32.7 %fusion.11 = f32[2,2048,640]{2,1,0:T(8,128)S(1)} fusion(f32[2,2048,640]{2,1,0:T(8,128)S(1)} %multiply_add_fusion, f32[2,640,640]{2,1,0:T(8,128)S(1)} %fusion.260, f32[2,640,640]{2,1,0:T(8,128)S(1)} %fusion.259), kind=kOutput, calls=%fused_computation.31 | convolution fusion | flops 20135116800 | bytes 27525120 | tf_op jit(solution)/shard_map/kri,kil->krl/dot_general | solution.py:288
  (653 shorter events, 321.0 us)
Async XLA Ops:
  7.2 171.1 %copy-start.196 = (u32[32]{0:T(128)S(1)}, u32[32]{0:T(128)}, u32[]{:S(2)}) copy-start(u32[32]{0:T(128)} %constant.616) | copy-start | bytes 388
  7.2 137.5 %copy-start.101 = (f32[64,640]{1,0:T(8,128)S(1)}, f32[64,640]{1,0:T(8,128)}, u32[]{:S(2)}) copy-start(f32[64,640]{1,0:T(8,128)} %param.32) | copy-start | bytes 491524
  7.2 171.0 %copy-start.190 = (f32[96]{0:T(128)S(1)}, f32[96]{0:T(128)}, u32[]{:S(2)}) copy-start(f32[96]{0:T(128)} %param.33) | copy-start | bytes 1156
  7.2 278.0 %all-gather.27.cloned.1.call-start = ((), (), s32[]{:S(2)}) async-start(), calls=%async_computation.4 | async-start | bytes 1638400 | tf_op jit(solution)/shard_map/all_gather | solution.py:254
  8.3 194.5 %copy-start.189 = (s32[2,256]{1,0:T(2,128)S(1)}, s32[2,256]{1,0:T(2,128)}, u32[]{:S(2)}) copy-start(s32[2,256]{1,0:T(2,128)} %param.25) | copy-start | bytes 6148
  8.3 194.7 %copy-start.123 = (f32[20,256]{1,0:T(8,128)S(1)}, f32[20,256]{1,0:T(8,128)}, u32[]{:S(2)}) copy-start(f32[20,256]{1,0:T(8,128)} %param.28) | copy-start | bytes 61444
  41.3 252.3 %all-gather.29.cloned.1.call-start = ((), (), s32[]{:S(2)}) async-start(), calls=%async_computation.5 | async-start | bytes 1638400 | tf_op jit(solution)/shard_map/all_gather | solution.py:257
  75.3 164.6 %copy-start.3 = (bf16[512,640]{1,0:T(8,128)(2,1)S(1)}, bf16[512,640]{1,0:T(8,128)(2,1)}, u32[]{:S(2)}) copy-start(bf16[512,640]{1,0:T(8,128)(2,1)} %param.23) | copy-start | bytes 1966084
  75.3 225.0 %all-gather.31.cloned.1.call-start = ((), (), s32[]{:S(2)}) async-start(), calls=%async_computation.6 | async-start | bytes 3276800 | tf_op jit(solution)/shard_map/all_gather | solution.py:258
  110.3 194.2 %all-gather.33.cloned.1.call-start = ((), (), s32[]{:S(2)}) async-start(), calls=%async_computation.7 | async-start | bytes 3276800 | tf_op jit(solution)/shard_map/all_gather | solution.py:259
  144.7 165.0 %all-gather.35.cloned.1.call-start = ((), (), s32[]{:S(2)}) async-start(), calls=%async_computation.8 | async-start | bytes 3276800 | tf_op jit(solution)/shard_map/all_gather | solution.py:260
  178.2 824.8 %reduce-scatter.2.cloned.1.call-start = ((), (), s32[]{:S(2)}) async-start(), calls=%async_computation.3 | async-start | bytes 43253760 | tf_op jit(solution)/shard_map/reduce_scatter | solution.py:421
  562.3 461.8 %copy-start.177 = (s32[8]{0:T(128)S(1)}, s32[8]{0:T(128)}, u32[]{:S(2)}) copy-start(s32[8]{0:T(128)} %copy-done.176) | copy-start | bytes 100
  562.3 462.4 %copy-start.192 = (s32[8]{0:T(128)S(1)}, s32[8]{0:T(128)}, u32[]{:S(2)}) copy-start(s32[8]{0:T(128)} %constant.584.clone) | copy-start | bytes 100
  562.3 466.0 %copy-start.83 = (bf16[256,256]{1,0:T(8,128)(2,1)S(1)}, bf16[256,256]{1,0:T(8,128)(2,1)}, u32[]{:S(2)}) copy-start(bf16[256,256]{1,0:T(8,128)(2,1)} %copy-done.82) | copy-start | bytes 393220
  562.4 466.0 %copy-start.44 = (bf16[8,80,256]{2,1,0:T(8,128)(2,1)S(1)}, bf16[8,80,256]{2,1,0:T(8,128)(2,1)}, u32[]{:S(2)}) copy-start(bf16[8,80,256]{2,1,0:T(8,128)(2,1)} %copy-done.43) | copy-start | bytes 983044
  562.4 466.3 %copy-start.46 = (bf16[8,80,256]{2,1,0:T(8,128)(2,1)S(1)}, bf16[8,80,256]{2,1,0:T(8,128)(2,1)}, u32[]{:S(2)}) copy-start(bf16[8,80,256]{2,1,0:T(8,128)(2,1)} %copy-done.45) | copy-start | bytes 983044
  562.4 466.3 %copy-start.81 = (bf16[256,256]{0,1:T(8,128)(2,1)S(1)}, bf16[256,256]{0,1:T(8,128)(2,1)}, u32[]{:S(2)}) copy-start(bf16[256,256]{0,1:T(8,128)(2,1)} %copy-done.80) | copy-start | bytes 393220
  562.4 466.6 %copy-start.85 = (bf16[256,256]{1,0:T(8,128)(2,1)S(1)}, bf16[256,256]{1,0:T(8,128)(2,1)}, u32[]{:S(2)}) copy-start(bf16[256,256]{1,0:T(8,128)(2,1)} %copy-done.84) | copy-start | bytes 393220
  562.4 467.0 %copy-start.79 = (bf16[256,256]{0,1:T(8,128)(2,1)S(1)}, bf16[256,256]{0,1:T(8,128)(2,1)}, u32[]{:S(2)}) copy-start(bf16[256,256]{0,1:T(8,128)(2,1)} %copy-done.78) | copy-start | bytes 393220
  562.4 532.7 %all-gather.37.cloned.1.call-start = ((), (), s32[]{:S(2)}) async-start(), calls=%async_computation.9 | async-start | bytes 5898240 | tf_op jit(solution)/shard_map/all_gather | solution.py:426
  1084.7 404.7 %copy-start.193 = (f32[96]{0:T(128)}, f32[96]{0:T(128)S(1)}, u32[]{:S(2)}) copy-start(f32[96]{0:T(128)S(1)} %get-tuple-element.60) | copy-start | bytes 1156
  1470.2 13.7 all-to-all-start
  1483.9 13.7 all-to-all-start.1
  (187 other events, 1772.2 us)
Sparse Core Ops, SparseCore 0:
  41.4 19.1 all-gather.26
  75.5 19.1 all-gather.28
  110.4 26.4 all-gather.30
  144.8 26.4 all-gather.32
  178.3 26.5 all-gather.34
  562.5 440.4 reduce-scatter.1
  1005.7 89.3 all-gather.36
where the time goes:
time: 1520 us; the launch traced here: 1510 us
  waiting for transfers between devices  459 us (30%)
  matrix products  448 us (29%)
  blocking collectives  312 us (21%)
  local copies, waits for them, and re-layouts  140 us (9%)
  other arithmetic  108 us (7%)
  between operations  36.5 us (2%)
    reduce_scatter x1, waiting for transfers between devices, shards(): lax.psum_scatter(routed, ('dp', 'fsdp'), scatter_dimension=0, tiled=True)  440 us
    dot_general x5, matrix products, newton_step(): jnp.einsum('kri,kil->krl', iterate, polynomial, precision=HIGHEST, prefer...  168 us
    dot_general x5, matrix products, shards(): jnp.einsum('kri,krj->kij', iterate, iterate, precision=HIGHEST, preferred...  143 us
    unnamed x2, blocking collectives  66 us
    unnamed x424, local copies, waits for them, and re-layouts  63.6 us
    gather x4, local copies, waits for them, and re-layouts, shards(): jnp.take(stacked, holder, axis=1).reshape(devices_all, slots, tile_rows, D)  62 us
    dot_general x5, matrix products, newton_step(): jnp.einsum('kij,kjl->kil', gram_matrix, gram_matrix, precision=HIGHEST, p...  47 us
    all_gather x1, blocking collectives, shards(): lax.all_gather(up_part, 'dp', axis=0, tiled=True)  34.2 us
  transfers between devices with their start and end apart: 9, of which 4 were waited for; matrix products, arithmetic and copies ran while one was open for 4% of the time, Pallas kernels for 0%

commit v1 on v0

v1 whole, which is shorter than its diff:
```python
import math

import jax
import jax.numpy as jnp
from jax import lax
from jax.sharding import PartitionSpec as P

D = 640
HEADS = 4
HD = 256
FF = 2048
NS_ITERS = 5


EPSILON = 1e-06
THETA = 1000000.0
MOMENTUM = 0.95
LEARN_RATE = 0.05
NS_FIRST = 3.4445
NS_SECOND = -4.775
NS_THIRD = 2.0315
HIGHEST = lax.Precision.HIGHEST
MASKED = -1e30


def dot_plain(left, right):
    return jnp.dot(left, right, preferred_element_type=jnp.float32)


def dot_right_t(left, right):
    return lax.dot_general(
        left, right, (((1,), (1,)), ((), ())), preferred_element_type=jnp.float32
    )


def dot_left_t(left, right):
    return lax.dot_general(
        left, right, (((0,), (0,)), ((), ())), preferred_element_type=jnp.float32
    )


def norm_rows(values, gain):
    return values * lax.rsqrt(jnp.mean(values * values, axis=-1, keepdims=True) + EPSILON) * gain


def rotary(values, cosine, sine):
    middle = values.shape[-1] // 2
    first_half = values[..., :middle]
    second_half = values[..., middle:]
    return jnp.concatenate(
        [first_half * cosine - second_half * sine, second_half * cosine + first_half * sine],
        axis=-1,
    )


def rotary_tables(segment, head_size):
    length = segment.shape[1]
    starts = jnp.sum((segment[:, None, :] < segment[:, :, None]).astype(jnp.int32), axis=2)
    places = (jnp.arange(length, dtype=jnp.int32)[None] - starts).astype(jnp.float32)
    frequency = jnp.exp(
        -math.log(THETA) * 2.0 * jnp.arange(head_size // 2, dtype=jnp.float32) / head_size
    )
    angles = places.reshape(-1)[:, None] * frequency[None, :]
    return (jnp.cos(angles), jnp.sin(angles))


def allowed_pairs(segment):
    length = segment.shape[1]
    positions = jnp.arange(length, dtype=jnp.int32)
    same_doc = segment[:, :, None] == segment[:, None, :]
    return jnp.logical_and(same_doc, (positions[None, :] <= positions[:, None])[None])


def split_gains(gain_vec, width, head_size):
    return (
        gain_vec[:width],
        gain_vec[width : 2 * width],
        gain_vec[2 * width : 3 * width],
        gain_vec[3 * width : 4 * width],
        gain_vec[4 * width : 4 * width + head_size],
        gain_vec[4 * width + head_size :],
    )


def query_rotated(query, gain, cosine, sine):
    length = query.shape[0]
    shaped = query.reshape(length, HEADS, query.shape[1] // HEADS)
    return rotary(norm_rows(shaped, gain), cosine[:, None, :], sine[:, None, :])


def key_rotated(key_rows, gain, cosine, sine):
    return rotary(norm_rows(key_rows, gain), cosine, sine)


def attention_scores(query_bf, key_bf, allowed):
    scale = query_bf.shape[-1] ** (-0.5)
    products = (
        jnp.einsum("bthd,bsd->bhts", query_bf, key_bf, preferred_element_type=jnp.float32) * scale
    )
    return jnp.where(allowed[:, None], products, MASKED)


def gelu_product(gate, upward):
    return jax.nn.gelu(gate, approximate=True) * upward


def block_step(rows_in, cot_rows, segment, weights, gain_vec):
    query_w, key_w, value_w, out_w, gate_w, up_w, down_w = weights
    batches, length = segment.shape
    total, width = rows_in.shape
    head_size = key_w.shape[1]
    gain_in, gain_attn, gain_ff, gain_post, gain_query, gain_key = split_gains(
        gain_vec, width, head_size
    )
    x_rows = rows_in.astype(jnp.float32)
    normed = norm_rows(x_rows, gain_in).astype(jnp.bfloat16)
    query = dot_right_t(normed, query_w)
    key_rows = dot_plain(normed, key_w)
    value = dot_plain(normed, value_w).astype(jnp.bfloat16)
    cosine, sine = rotary_tables(segment, head_size)
    query_bf = query_rotated(query, gain_query, cosine, sine).astype(jnp.bfloat16)
    query_bf = query_bf.reshape(batches, length, HEADS, head_size)
    key_bf = key_rotated(key_rows, gain_key, cosine, sine).astype(jnp.bfloat16)
    key_bf = key_bf.reshape(batches, length, head_size)
    value_b = value.reshape(batches, length, head_size)
    allowed = allowed_pairs(segment)
    scores = attention_scores(query_bf, key_bf, allowed)
    peak = jnp.max(scores, axis=-1, keepdims=True)
    log_total = peak + jnp.log(jnp.sum(jnp.exp(scores - peak), axis=-1, keepdims=True))
    probs_full = jnp.exp(scores - log_total)
    probs = probs_full.astype(jnp.bfloat16)
    mixed = jnp.einsum("bhts,bsd->bthd", probs, value_b, preferred_element_type=jnp.float32)
    mixed = mixed.astype(jnp.bfloat16).reshape(total, -1)
    attn = dot_plain(mixed, out_w)
    hidden = x_rows + norm_rows(attn, gain_attn)
    ff_in = norm_rows(hidden, gain_ff).astype(jnp.bfloat16)
    gate = dot_right_t(ff_in, gate_w)
    upward = dot_right_t(ff_in, up_w)
    act = gelu_product(gate, upward).astype(jnp.bfloat16)
    ff_out = dot_plain(act, down_w)
    result = (hidden + norm_rows(ff_out, gain_post)).astype(jnp.bfloat16)

    d_output = cot_rows.astype(jnp.float32)
    unused, pullback = jax.vjp(norm_rows, ff_out, gain_post)
    d_ffout, dg_post = pullback(d_output)
    d_ffout = d_ffout.astype(jnp.bfloat16)
    down_grad = dot_left_t(act, d_ffout)
    d_act = dot_right_t(d_ffout, down_w)
    unused, pullback = jax.vjp(gelu_product, gate, upward)
    d_gate, d_upward = pullback(d_act)
    d_gate = d_gate.astype(jnp.bfloat16)
    d_upward = d_upward.astype(jnp.bfloat16)
    gate_grad = dot_left_t(d_gate, ff_in)
    up_grad = dot_left_t(d_upward, ff_in)
    d_ffin = dot_plain(d_gate, gate_w) + dot_plain(d_upward, up_w)
    unused, pullback = jax.vjp(norm_rows, hidden, gain_ff)
    d_inner, dg_ff = pullback(d_ffin)
    d_hidden = d_output + d_inner
    unused, pullback = jax.vjp(norm_rows, attn, gain_attn)
    d_attn, dg_attn = pullback(d_hidden)
    d_attn = d_attn.astype(jnp.bfloat16)
    out_grad = dot_left_t(mixed, d_attn)
    d_mixed = dot_right_t(d_attn, out_w).astype(jnp.bfloat16)
    d_mixed = d_mixed.reshape(batches, length, HEADS, head_size)
    d_value = jnp.einsum(
        "bhts,bthd->bsd", probs, d_mixed, preferred_element_type=jnp.float32
    ).astype(jnp.bfloat16)
    d_probs = jnp.einsum("bthd,bsd->bhts", d_mixed, value_b, preferred_element_type=jnp.float32)
    row_dot = jnp.sum(probs_full * d_probs, axis=-1, keepdims=True)
    d_scores = (probs_full * (d_probs - row_dot) * head_size ** (-0.5)).astype(jnp.bfloat16)
    d_qrot = jnp.einsum("bhts,bsd->bthd", d_scores, key_bf, preferred_element_type=jnp.float32)
    d_krot = jnp.einsum("bhts,bthd->bsd", d_scores, query_bf, preferred_element_type=jnp.float32)
    d_qrot = d_qrot.reshape(total, HEADS, head_size)
    d_krot = d_krot.reshape(total, head_size)
    d_value = d_value.reshape(total, head_size)
    unused, pullback = jax.vjp(
        lambda values, gain: query_rotated(values, gain, cosine, sine), query, gain_query
    )
    d_query, dg_query = pullback(d_qrot)
    unused, pullback = jax.vjp(
        lambda values, gain: key_rotated(values, gain, cosine, sine), key_rows, gain_key
    )
    d_key, dg_key = pullback(d_krot)
    d_query = d_query.astype(jnp.bfloat16)
    d_key = d_key.astype(jnp.bfloat16)
    query_grad = dot_left_t(d_query, normed)
    key_grad = dot_left_t(normed, d_key)
    value_grad = dot_left_t(normed, d_value)
    d_normed = (
        dot_plain(d_query, query_w) + dot_right_t(d_key, key_w) + dot_right_t(d_value, value_w)
    )
    unused, pullback = jax.vjp(norm_rows, x_rows, gain_in)
    d_inputs, dg_in = pullback(d_normed)
    grad_rows = (d_hidden + d_inputs).astype(jnp.bfloat16)
    gain_grad = jnp.concatenate([dg_in, dg_attn, dg_ff, dg_post, dg_query, dg_key])
    grads = (query_grad, key_grad, value_grad, out_grad, gate_grad, up_grad, down_grad)
    return (result, grad_rows, grads, gain_grad)


def dot_fine(left, right):
    return jnp.dot(
        left, right, precision=lax.Precision.HIGH, preferred_element_type=jnp.float32
    )


def polar_factor(rows_all):
    gram = dot_left_t(rows_all, rows_all)
    size = gram.shape[0]
    eye = jnp.arange(size)[:, None] == jnp.arange(size)[None, :]
    inverse = 1.0 / (jnp.sqrt(jnp.sum(jnp.where(eye, gram, 0.0))) + 1e-07)
    gram = gram * (inverse * inverse)
    product = None
    for iteration in range(NS_ITERS):
        square = dot_fine(gram, gram)
        poly = NS_SECOND * gram + NS_THIRD * square + jnp.where(eye, NS_FIRST, 0.0)
        product = poly if product is None else dot_fine(product, poly)
        if iteration + 1 < NS_ITERS:
            cubic = NS_FIRST * gram + NS_SECOND * square + NS_THIRD * dot_fine(gram, square)
            gram = dot_fine(cubic, poly)
    return product * inverse


def as_rows(shard, width):
    return shard.reshape(-1, width)


def pad_to(piece, rows, cols):
    return jnp.pad(piece, ((0, rows - piece.shape[0]), (0, cols - piece.shape[1])))


def shards(
    tokens,
    cotangent,
    segments,
    query_weight,
    key_weight,
    value_weight,
    out_weight,
    gate_weight,
    up_weight,
    down_weight,
    norm_gains,
    query_state,
    key_state,
    value_state,
    out_state,
    gate_state,
    up_state,
    down_state,
    gains_state,
):
    axes = ("dp", "fsdp")
    groups = lax.axis_size("dp")
    devices_all = lax.axis_size("fsdp") * groups
    width = tokens.shape[1]
    masters = (
        query_weight,
        key_weight,
        value_weight,
        out_weight,
        gate_weight,
        up_weight,
        down_weight,
    )
    states = (query_state, key_state, value_state, out_state, gate_state, up_state, down_state)
    sizes = [matrix.size // width for matrix in masters]
    starts = [sum(sizes[:number]) for number in range(8)]
    gain_rows = norm_gains.shape[0]
    padded_rows = -(-(starts[7] + 1) // 16) * 16

    def pack(pieces, gains, lead):
        filler = jnp.zeros(lead + ((padded_rows - starts[7]) * width - gain_rows,), jnp.bfloat16)
        last = jnp.concatenate([gains, filler], axis=-1)
        last = last.reshape(lead + (padded_rows - starts[7], width))
        return jnp.concatenate(list(pieces) + [last], axis=len(lead))

    packed = pack(
        [as_rows(matrix.astype(jnp.bfloat16), width) for matrix in masters],
        norm_gains.astype(jnp.bfloat16),
        (),
    )
    gathered = lax.all_gather(packed, axes, axis=0, tiled=False)
    weights = tuple(
        gathered[:, starts[number] : starts[number + 1]].reshape(-1, masters[number].shape[1])
        for number in range(7)
    )
    gain_vec = gathered[:, starts[7], :gain_rows].reshape(-1).astype(jnp.float32)
    block_out, tokens_grad, grads, gain_grad = block_step(
        tokens, cotangent, segments, weights, gain_vec
    )
    sends = pack(
        [grad.astype(jnp.bfloat16).reshape(devices_all, -1, width) for grad in grads],
        gain_grad.astype(jnp.bfloat16).reshape(devices_all, gain_rows),
        (devices_all,),
    )
    summed = lax.psum_scatter(
        sends.reshape(devices_all * padded_rows, width), axes, scatter_dimension=0, tiled=True
    )
    grad_list = [
        summed[starts[number] : starts[number + 1]]
        .reshape(masters[number].shape)
        .astype(jnp.float32)
        for number in range(7)
    ]
    gains_grad = summed[starts[7], :gain_rows].astype(jnp.float32)
    moments = [MOMENTUM * state + grad for state, grad in zip(states, grad_list)]
    gains_moment = MOMENTUM * gains_state + gains_grad

    slots = -(-7 // groups)
    tile = max(matrix.shape[0] for matrix in masters)
    blank = jnp.zeros((tile, width), jnp.bfloat16)
    chunks = [pad_to(moment.astype(jnp.bfloat16), tile, width) for moment in moments]
    chunks = chunks + [blank] * (groups * slots - 7)
    outgoing = jnp.stack(chunks, axis=0)
    mine = lax.all_to_all(outgoing, "dp", split_axis=0, concat_axis=0, tiled=True)
    mine = mine.reshape(groups, slots, tile, width).swapaxes(0, 1).reshape(slots, -1, width)
    whole = lax.all_gather(mine, "fsdp", axis=1, tiled=True)
    ortho = []
    for place in range(slots):
        factor = polar_factor(whole[place]).astype(jnp.bfloat16)
        ortho.append(dot_plain(mine[place], factor).astype(jnp.bfloat16))
    ortho = jnp.stack(ortho, axis=0).reshape(slots, groups, tile, width).swapaxes(0, 1)
    back = lax.all_to_all(
        ortho.reshape(groups * slots, tile, width), "dp", split_axis=0, concat_axis=0, tiled=True
    )
    updated = []
    for number in range(7):
        rows_here, cols_here = masters[number].shape
        scale = LEARN_RATE * 0.2 * math.sqrt(max(rows_here * devices_all, cols_here))
        turned = back[number, :rows_here, :cols_here].astype(jnp.float32)
        updated.append(masters[number] - scale * turned)
    tokens_all = tokens.shape[0] * devices_all
    gains_new = norm_gains - 0.1 / math.sqrt(tokens_all) * gains_moment
    return (
        block_out,
        tokens_grad,
        *grad_list,
        gains_grad,
        *updated,
        gains_new,
        *moments,
        gains_moment,
    )


def solution(mesh):
    return jax.shard_map(
        shards,
        mesh=mesh,
        in_specs=(
            P(("dp", "fsdp"), None),
            P(("dp", "fsdp"), None),
            P(("dp", "fsdp"), None),
            P(("dp", "fsdp"), None),
            P(("dp", "fsdp"), None),
            P(("dp", "fsdp"), None),
            P(("dp", "fsdp"), None),
            P(("dp", "fsdp"), None),
            P(("dp", "fsdp"), None),
            P(("dp", "fsdp"), None),
            P(("dp", "fsdp")),
            P(("dp", "fsdp"), None),
            P(("dp", "fsdp"), None),
            P(("dp", "fsdp"), None),
            P(("dp", "fsdp"), None),
            P(("dp", "fsdp"), None),
            P(("dp", "fsdp"), None),
            P(("dp", "fsdp"), None),
            P(("dp", "fsdp")),
        ),
        out_specs=(
            P(("dp", "fsdp"), None),
            P(("dp", "fsdp"), None),
            P(("dp", "fsdp"), None),
            P(("dp", "fsdp"), None),
            P(("dp", "fsdp"), None),
            P(("dp", "fsdp"), None),
            P(("dp", "fsdp"), None),
            P(("dp", "fsdp"), None),
            P(("dp", "fsdp"), None),
            P(("dp", "fsdp")),
            P(("dp", "fsdp"), None),
            P(("dp", "fsdp"), None),
            P(("dp", "fsdp"), None),
            P(("dp", "fsdp"), None),
            P(("dp", "fsdp"), None),
            P(("dp", "fsdp"), None),
            P(("dp", "fsdp"), None),
            P(("dp", "fsdp")),
            P(("dp", "fsdp"), None),
            P(("dp", "fsdp"), None),
            P(("dp", "fsdp"), None),
            P(("dp", "fsdp"), None),
            P(("dp", "fsdp"), None),
            P(("dp", "fsdp"), None),
            P(("dp", "fsdp"), None),
            P(("dp", "fsdp")),
        ),
        check_vma=False,
    )
```

time: 1520 us -> 522 us (0.34)
  matrix products: 448 us -> 120 us
  blocking collectives: 312 us -> 19 us
  waiting for transfers between devices: 459 us -> 275 us
  local copies, waits for them, and re-layouts: 140 us -> 43.7 us
  other arithmetic: 108 us -> 36.5 us
  between operations: 36.5 us -> 16 us
    dot_general x27 -> x23, matrix products: 376 us -> 64.2 us  [the longest x17 44.4 us: dot_fine(): jnp.dot(left, right, precision=lax.Precision.HIGH, preferred_element_type...]
    reduce_scatter x1, waiting for transfers between devices: 440 us -> 147 us  [shards(): lax.psum_scatter(sends.reshape(devices_all * padded_rows, width), axes, s...]
    all_gather x10 -> x0, blocking collectives: 246 us -> none  [the longest x1 34.2 us: shards(): lax.all_gather(up_part, 'dp', axis=0, tiled=True)]
    all_gather x6 -> x2, waiting for transfers between devices: 6.68 us -> 115 us  [the longest x1 88.8 us: shards(): gathered = lax.all_gather(packed, axes, axis=0, tiled=False)]
    gather x8 -> x0, local copies, waits for them, and re-layouts: 68.2 us -> none  [the longest x4 62 us: shards(): jnp.take(stacked, holder, axis=1).reshape(devices_all, slots, tile_rows, D)]
    unnamed x2 -> x0, blocking collectives: 66 us -> none
    unnamed x424 -> x205, local copies, waits for them, and re-layouts: 63.6 us -> 22.8 us
    select_n x4 -> x0, other arithmetic: 29.5 us -> none  [the longest x2 29.5 us: shards(): jnp.take(stacked, holder, axis=1).reshape(devices_all, slots, tile_rows, D)]
  transfers between devices with their start and end apart: 9 -> 4, of which waited for: 4 -> 4; matrix products, arithmetic and copies ran while one was open for 4% -> 1% of each run, Pallas kernels for 0% -> 0%
where the time goes in v1:
time: 522 us; the launch traced here: 517 us
  waiting for transfers between devices  275 us (53%)
  matrix products  120 us (23%)
  local copies, waits for them, and re-layouts  43.7 us (8%)
  other arithmetic  36.5 us (7%)
  blocking collectives  19 us (4%)
  between operations  16 us (3%)
  starting transfers between devices  6.12 us (1%)
    reduce_scatter x1, waiting for transfers between devices, shards(): lax.psum_scatter(sends.reshape(devices_all * padded_rows, width), axes, s...  147 us
    all_gather x1, waiting for transfers between devices, shards(): gathered = lax.all_gather(packed, axes, axis=0, tiled=False)  88.8 us
    dot_general x17, matrix products, dot_fine(): jnp.dot(left, right, precision=lax.Precision.HIGH, preferred_element_type...  44.4 us
    all_gather x1, waiting for transfers between devices, shards(): whole = lax.all_gather(mine, 'fsdp', axis=1, tiled=True)  26.1 us
    dot_general x7, matrix products, dot_right_t(): lax.dot_general(left, right, (((1,), (1,)), ((), ())), preferred_element_...  25.7 us
    unnamed x205, local copies, waits for them, and re-layouts  22.8 us
    dot_general x8, matrix products, dot_left_t(): lax.dot_general(left, right, (((0,), (0,)), ((), ())), preferred_element_...  19.6 us
    all_to_all x1, blocking collectives, shards(): lax.all_to_all(outgoing, 'dp', split_axis=0, concat_axis=0, tiled=True)  19 us
  transfers between devices with their start and end apart: 4, of which 4 were waited for; matrix products, arithmetic and copies ran while one was open for 1% of the time, Pallas kernels for 0%

profile of v1, /device:TPU:26, one launch (start us, length us, event | category | flops | bytes accessed | tf_op | source)
XLA Modules:
  0.0 517.1 jit_solution(9548593773665804449)
XLA Ops:
  17.6 88.8 %all-gather.6.cloned.1.call-done = bf16[9216,640]{1,0:T(8,128)(2,1)} async-done(((bf16[288,640]{1,0:T(8,128)(2,1)}), bf16[9216,640]{1,0:T(8,128)(2,1)}) %all-gather.6.cloned.1.call-update) | async-done | bytes 11796496 | tf_op jit(solution)/shard_map/all_gather | solution.py:282
  109.1 3.5 fusion.195
  112.6 5.5 %fusion.194 = (bf16[32,64,640]{2,1,0:T(8,128)(2,1)}, bf16[32,64,640]{2,1,0:T(8,128)(2,1)}, bf16[32,64,640]{2,1,0:T(8,128)(2,1)}) fusion(bf16[32,288,640]{2,1,0:T(8,128)(2,1)} %bitcast.191), kind=kLoop, calls=%fused_computation.325 | loop fusion | bytes 15728640 | tf_op jit(solution)/shard_map/slice | solution.py:284
  128.5 2.7 copy.57
  144.3 16.3 %multiply_convert_fusion = (bf16[512,2048]{1,0:T(8,128)(2,1)S(1)}, bf16[512,2048]{1,0:T(8,128)(2,1)S(1)}) fusion(f32[512,2048]{1,0:T(8,128)S(1)} %fusion.200, f32[512,2048]{1,0:T(8,128)S(1)} %get-tuple-element.111, bf16[512,640]{1,0:T(8,128)(2,1)S(1)} %get-tuple-element.76, bf16[2048,640]{1,0:T(8,128)(2,1)S(1)} %bitcast.206), kind=kOutput, calls=%fused_computation.10 | convolution fusion | flops 1367343104 | bytes 15859712 | tf_op jit(solution)/shard_map/dot_general | solution.py:31
  172.6 3.1 fusion.79
  175.7 6.0 %convolution_bitcast_fusion = f32[2,256,4,256]{3,1,2,0:T(8,128)} fusion(f32[2,256,256,4]{2,1,3,0:T(8,128)} %fusion.79, f32[2,4,256,256]{2,3,1,0:T(8,128)} %copy-done, f32[2,4,256]{2,1,0:T(4,128)S(1)} %bitcast.232, bf16[2,256,128]{2,1,0:T(8,128)(2,1)} %bitcast.230, bf16[2,256,128]{2,1,0:T(8,128)(2,1)S(1)} %bitcast.228), kind=kOutput, calls=%fused_computation.84 | convolution fusion | flops 272632064 | bytes 6561792 | tf_op jit(solution)/shard_map/bhts,bsd->bthd/dot_general | solution.py:171
  181.7 5.5 %fusion.47 = f32[2,256,256,1]{2,1,3,0:T(8,128)} fusion(f32[2,256,256,4]{2,1,3,0:T(8,128)} %fusion.79, f32[2,4,256,256]{2,3,1,0:T(8,128)} %copy-done, f32[2,4,256]{2,1,0:T(4,128)S(1)} %bitcast.233, bf16[2,256,4,128]{3,1,0,2:T(8,128)(2,1)} %bitcast.225, bf16[2,256,4,128]{3,1,0,2:T(8,128)(2,1)} %bitcast.223), kind=kOutput, calls=%fused_computation.87 | convolution fusion | flops 274204928 | bytes 5775360 | tf_op jit(solution)/shard_map/bhts,bthd->bsd/dot_general | solution.py:172
  187.2 3.2 fusion.69
  192.6 3.3 convolution_convert_fusion.2
  195.9 3.3 convolution_convert_fusion.1
  199.3 3.3 convolution_convert_fusion
  231.2 147.5 %reduce-scatter.2.cloned.1.call-done = bf16[288,640]{1,0:T(8,128)(2,1)} async-done(((bf16[9216,640]{1,0:T(8,128)(2,1)}), bf16[288,640]{1,0:T(8,128)(2,1)}) %reduce-scatter.2.cloned.1.call-update) | async-done | bytes 368656 | tf_op jit(solution)/shard_map/reduce_scatter | solution.py:296
  386.7 19.0 %all_to_all.10 = bf16[8,64,640]{2,1,0:T(8,128)(2,1)} all-to-all(bf16[8,64,640]{2,1,0:T(8,128)(2,1)S(1)} %constant_dynamic-update-slice_fusion.13), channel_id=1, replica_groups=mesh['dp'=8,'fsdp'=4] {'dp'}, dimensions={0} | all-to-all | bytes 1310720 | tf_op jit(solution)/shard_map/all_to_all | solution.py:315
  405.7 26.1 %all-gather.4.cloned.1.call-done = bf16[1,2048,640]{2,1,0:T(8,128)(2,1)} async-done(((bf16[1,512,640]{2,1,0:T(8,128)(2,1)}), bf16[1,2048,640]{2,1,0:T(8,128)(2,1)}) %all-gather.4.cloned.1.call-update) | async-done | bytes 2621456 | tf_op jit(solution)/shard_map/all_gather | solution.py:317
  431.8 5.4 %select_reduce_fusion = (f32[]{:T(128)}, f32[640,640]{1,0:T(8,128)S(1)}) fusion(bf16[1,2048,640]{2,1,0:T(8,128)(2,1)} %all-gather.4.cloned.1.call-done), kind=kOutput, calls=%fused_computation.82 | convolution fusion | flops 1678950400 | bytes 4259844 | tf_op jit(solution)/shard_map/dot_general | solution.py:37
  442.8 2.9 fusion.39
  448.1 2.9 fusion.38
  453.5 2.8 fusion.32
  458.8 2.9 fusion.206
  464.2 2.8 fusion.25
  474.6 2.8 fusion.18
  484.0 6.0 %all-to-all-start.1 = ((bf16[8,64,640]{2,1,0:T(8,128)(2,1)}), bf16[8,64,640]{2,1,0:T(8,128)(2,1)}, u32[]{:S(2)}, u32[]{:S(2)}) async-start(bf16[8,64,640]{2,1,0:T(8,128)(2,1)} %bitcast.221), calls=%async_computation.2 | async-start | bytes 1310720 | tf_op jit(solution)/shard_map/all_to_all | solution.py:323
  492.5 12.9 %all-to-all-done.1 = bf16[8,64,640]{2,1,0:T(8,128)(2,1)} async-done(((bf16[8,64,640]{2,1,0:T(8,128)(2,1)}), bf16[8,64,640]{2,1,0:T(8,128)(2,1)}, u32[]{:S(2)}, u32[]{:S(2)}) %all-to-all-start.1) | async-done | bytes 655392 | tf_op jit(solution)/shard_map/all_to_all | solution.py:323
  (322 shorter events, 122.6 us)
Async XLA Ops:
  7.2 9.6 %copy-start.63 = (s32[2,256]{1,0:T(2,128)S(1)}, s32[2,256]{1,0:T(2,128)}, u32[]{:S(2)}) copy-start(s32[2,256]{1,0:T(2,128)} %param.21) | copy-start | bytes 6148
  7.2 9.3 %copy-start.1 = (bf16[512,640]{1,0:T(8,128)(2,1)S(1)}, bf16[512,640]{1,0:T(8,128)(2,1)}, u32[]{:S(2)}) copy-start(bf16[512,640]{1,0:T(8,128)(2,1)} %param.19) | copy-start | bytes 1966084
  7.2 99.2 %all-gather.6.cloned.1.call-start = ((), (), s32[]{:S(2)}) async-start(), calls=%async_computation.5 | async-start | bytes 12165120 | tf_op jit(solution)/shard_map/all_gather | solution.py:282
  15.0 363.7 %reduce-scatter.2.cloned.1.call-start = ((), (), s32[]{:S(2)}) async-start(), calls=%async_computation.3 | async-start | bytes 12165120 | tf_op jit(solution)/shard_map/reduce_scatter | solution.py:296
  16.0 106.3 %copy-start.68 = (f32[1,2,2,128]{3,1,2,0:T(2,128)}, f32[1,2,2,128]{3,1,2,0:T(2,128)S(1)}, u32[]{:S(2)}) copy-start(f32[1,2,2,128]{3,1,2,0:T(2,128)S(1)} %copy.73) | copy-start | bytes 6148
  16.7 95.8 %copy-start.70 = (f32[512]{0:T(512)}, f32[512]{0:T(512)S(1)}, u32[]{:S(2)}) copy-start(f32[512]{0:T(512)S(1)} %fusion.67) | copy-start | bytes 6148
  16.8 103.3 %copy-start.66 = (f32[512]{0:T(512)}, f32[512]{0:T(512)S(1)}, u32[]{:S(2)}) copy-start(f32[512]{0:T(512)S(1)} %fusion.138) | copy-start | bytes 6148
  109.1 11.0 %copy-start.56 = (f32[640]{0:T(1024)}, f32[640]{0:T(1024)S(1)}, u32[]{:S(2)}) copy-start(f32[640]{0:T(1024)S(1)} %get-tuple-element.97) | copy-start | bytes 7684
  109.1 12.6 %copy-start.72 = (f32[256]{0:T(256)}, f32[256]{0:T(256)S(1)}, u32[]{:S(2)}) copy-start(f32[256]{0:T(256)S(1)} %get-tuple-element.98) | copy-start | bytes 3076
  109.1 14.3 %copy-start.74 = (f32[256]{0:T(256)}, f32[256]{0:T(256)S(1)}, u32[]{:S(2)}) copy-start(f32[256]{0:T(256)S(1)} %get-tuple-element.99) | copy-start | bytes 3076
  144.3 16.3 %copy-start.32 = (bf16[512,640]{1,0:T(8,128)(2,1)}, bf16[512,640]{1,0:T(8,128)(2,1)S(1)}, u32[]{:S(2)}) copy-start(bf16[512,640]{1,0:T(8,128)(2,1)S(1)} %get-tuple-element.76) | copy-start | bytes 1966084
  231.1 148.4 %copy-start.52 = (f32[32,640]{1,0:T(8,128)S(1)}, f32[32,640]{1,0:T(8,128)}, u32[]{:S(2)}) copy-start(f32[32,640]{1,0:T(8,128)} %param.33) | copy-start | bytes 245764
  231.1 148.4 %copy-start.53 = (f32[32,640]{1,0:T(8,128)S(1)}, f32[32,640]{1,0:T(8,128)}, u32[]{:S(2)}) copy-start(f32[32,640]{1,0:T(8,128)} %param.30) | copy-start | bytes 245764
  231.1 149.9 %copy-start.64 = (f32[20,256]{1,0:T(8,128)S(1)}, f32[20,256]{1,0:T(8,128)}, u32[]{:S(2)}) copy-start(f32[20,256]{1,0:T(8,128)} %param.32) | copy-start | bytes 61444
  231.1 150.0 %copy-start.65 = (f32[20,256]{1,0:T(8,128)S(1)}, f32[20,256]{1,0:T(8,128)}, u32[]{:S(2)}) copy-start(f32[20,256]{1,0:T(8,128)} %param.31) | copy-start | bytes 61444
  231.1 150.6 %copy-start.44 = (f32[64,640]{1,0:T(8,128)S(1)}, f32[64,640]{1,0:T(8,128)}, u32[]{:S(2)}) copy-start(f32[64,640]{1,0:T(8,128)} %param.34) | copy-start | bytes 491524
  231.1 152.3 %copy-start.45 = (f32[64,640]{1,0:T(8,128)S(1)}, f32[64,640]{1,0:T(8,128)}, u32[]{:S(2)}) copy-start(f32[64,640]{1,0:T(8,128)} %param.35) | copy-start | bytes 491524
  231.1 153.9 %copy-start.46 = (f32[64,640]{1,0:T(8,128)S(1)}, f32[64,640]{1,0:T(8,128)}, u32[]{:S(2)}) copy-start(f32[64,640]{1,0:T(8,128)} %param.36) | copy-start | bytes 491524
  231.1 200.7 %all-gather.4.cloned.1.call-start = ((), (), s32[]{:S(2)}) async-start(), calls=%async_computation.4 | async-start | bytes 3276800 | tf_op jit(solution)/shard_map/all_gather | solution.py:317
  482.4 7.6 %copy-start.3 = (bf16[512,640]{1,0:T(8,128)(2,1)S(1)}, bf16[512,640]{1,0:T(8,128)(2,1)}, u32[]{:S(2)}) copy-start(bf16[512,640]{1,0:T(8,128)(2,1)} %param.19) | copy-start | bytes 1966084
  484.0 21.4 %all-to-all-start.1 = ((bf16[8,64,640]{2,1,0:T(8,128)(2,1)}), bf16[8,64,640]{2,1,0:T(8,128)(2,1)}, u32[]{:S(2)}, u32[]{:S(2)}) async-start(bf16[8,64,640]{2,1,0:T(8,128)(2,1)} %bitcast.221), calls=%async_computation.2 | async-start | bytes 1310720 | tf_op jit(solution)/shard_map/all_to_all | solution.py:323
  490.1 15.4 %copy-start.43 = (f32[32,640]{1,0:T(8,128)S(1)}, f32[32,640]{1,0:T(8,128)}, u32[]{:S(2)}) copy-start(f32[32,640]{1,0:T(8,128)} %param.22) | copy-start | bytes 245764
  490.1 17.0 %copy-start.49 = (f32[20,256]{1,0:T(8,128)S(1)}, f32[20,256]{1,0:T(8,128)}, u32[]{:S(2)}) copy-start(f32[20,256]{1,0:T(8,128)} %param.23) | copy-start | bytes 61444
  490.1 18.3 %copy-start.36 = (f32[64,640]{1,0:T(8,128)S(1)}, f32[64,640]{1,0:T(8,128)}, u32[]{:S(2)}) copy-start(f32[64,640]{1,0:T(8,128)} %param.26) | copy-start | bytes 491524
  (72 other events, 151.0 us)
Sparse Core Ops, SparseCore 0:
  15.1 91.2 all-gather.5
  231.2 147.3 reduce-scatter.1
  405.9 25.8 all-gather.3
